TPU v7x, 512 devices: a whole 4x4x16 slice. The times are simulated.
512 devices in a mesh: sector: 32 (over z, core), cap: 16 (over y, x).
Axes of the slice: x: 4, y: 4, z: 16, core: 2. Of those that a mesh axis runs over, the one named last changes fastest.
Arguments:
- start_value: float32 [256, 32, 2048], P('sector', None, 'cap'), may hold values from 0 to 4
- firm_mass: float32 [256, 32, 2048], P('sector', None, 'cap'), may hold values from 0.1 to 10
- survive: int32 [256, 32, 2048], P('sector', None, 'cap'), may hold values from 0 to 1, as said below
- exit_index: int32 [256], P('sector'), may hold values from 0 to 8
- demand: float32 [256], P('sector'), may hold values from 0.3 to 90, as said below
- transition: float32 [32, 32], replicated, may hold values from 0 to 1, as said below
- install_cost: float32 [2048], P('cap'), may hold values from 0 to 1
Outputs:
- final_value: float32 [256, 32, 2048], P('sector', None, 'cap')
- rel_prices: float32 [256], P('sector')
Inputs may be any that keep to these rules, and one draw needn't show every extreme that they name: `survive`: 0 or 1; the share of ones differs from sector to sector, from about a tenth to all. `demand`: positive, rising over the sectors by some thirty times. `transition`: entries positive, every row sums to one.
All inputs are finite; a program needn't handle non-finite values.
Results may differ from a plain program's by a relative error of at most 0.0003.
Values sent between devices are 32-bit elements; how exact they have to be, the bound alone decides.
A program may use at most 64 MiB of HBM per device.

v0:
```python
import functools
import math

import jax
import jax.numpy as jnp
from jax import lax
from jax.sharding import Mesh
from jax.sharding import PartitionSpec as P

K = 2048
Z = 32
SWEEPS = 2
CAP = ("cap_0", "cap_1")


def over_axes(x, axes):
    return functools.reduce(lax.psum, axes, x)


def from_everyone(x, axis):
    copies = jnp.broadcast_to(x, (lax.axis_size(axis), *x.shape))
    return lax.all_to_all(copies, axis, split_axis=0, concat_axis=0, tiled=True)


def over_copies(x, axis):
    return from_everyone(x, axis).sum(axis=0)


def exchange_in_groups(x, axis, split_dim, concat_dim, work, item_dim, out_dim):
    items = jax.tree.leaves(x)[0].shape[item_dim]
    count = 2 if items % 2 == 0 else 1
    done = []
    for k in range(count):
        group = jax.tree.map(
            lambda a: lax.slice_in_dim(
                a, k * (items // count), (k + 1) * (items // count), axis=item_dim
            ),
            x,
        )
        done.append(
            work(
                lax.all_to_all(
                    group, axis, split_axis=split_dim, concat_axis=concat_dim, tiled=True
                )
            )
        )
    return jax.tree.map(lambda *parts: jnp.concatenate(parts, axis=out_dim), *done)


def capital_of(positions):
    return 0.2 * jnp.exp(jnp.log(10.0) * positions.astype(jnp.float32) / (K - 1))


def charge_of(cap_now, cap_next, row_ids, col_ids):
    invest = cap_next - 0.9 * cap_now
    fixed = jnp.where(row_ids == col_ids, 0.0, 1.5 * cap_now)
    return invest + invest * invest / cap_now + fixed


def best_reply(forward_rows, row_first, row_count, col_first):
    total_rows, total_cols = forward_rows.shape
    col_block = math.gcd(total_cols, 2048)
    row_block = math.gcd(row_count, 512)
    grp_limit = max(1, (1 << 24) // (row_block * col_block))
    grp_size = math.gcd(total_rows, 1 << min(total_rows, grp_limit).bit_length() - 1)
    groups = forward_rows.reshape(total_rows // grp_size, grp_size, total_cols)

    def one_group(group):

        def row_step(row_pos):
            row_ids = row_first + row_pos * row_block + jnp.arange(row_block, dtype=jnp.int32)
            cap_rows = capital_of(row_ids)
            empty = jnp.full((grp_size, row_block), -1e30, jnp.float32)
            col_ids = col_first + 0 * col_block + jnp.arange(col_block, dtype=jnp.int32)
            cap_cols = capital_of(col_ids)
            charge = charge_of(
                cap_rows[:, None], cap_cols[None, :], row_ids[:, None], col_ids[None, :]
            )
            return jnp.maximum(empty, jnp.max(group[:, None, :] - charge[None], axis=2))

        row_steps = row_count // row_block
        pieces = lax.map(row_step, jnp.arange(row_steps, dtype=jnp.int32))
        return pieces.transpose(1, 0, 2).reshape(grp_size, row_count)

    if total_rows == grp_size:
        return one_group(groups[0])
    return lax.map(one_group, groups).reshape(total_rows, row_count)


def on_device(start_value, firm_mass, survive, exit_index, demand, transition, install_cost):
    sec_dev, prod_count, cap_dev = start_value.shape
    sectors_all = sec_dev * lax.axis_size("sector")
    row_first = lax.axis_index(CAP) * cap_dev
    prod_index = jnp.arange(prod_count, dtype=jnp.int32)
    capital = capital_of(row_first + jnp.arange(cap_dev, dtype=jnp.int32))
    log_prod = -0.5 + prod_index.astype(jnp.float32) / (prod_count - 1)
    output = jnp.exp(log_prod)[:, None] * capital[None, :] ** 0.6
    scrap = 0.3 * capital
    live = (survive == 1) & (prod_index[None, :, None] >= exit_index[:, None, None])
    values = start_value
    relative = jnp.zeros((sec_dev,), jnp.float32)
    for sweep in range(SWEEPS):
        staying = jnp.where(live, jax.nn.sigmoid((values - scrap) / 0.5), 0.0)
        partial_value = jnp.sum(firm_mass * staying * output, axis=(1, 2))
        supply = 1.0 + over_axes(partial_value, CAP) / (Z * K)
        prices = jnp.sqrt(demand / supply)
        root_sum = over_copies(jnp.sum(jnp.sqrt(prices)), "sector")
        price_index = (root_sum / sectors_all) ** 2
        relative = prices / price_index
        continuation = jnp.where(live, jnp.maximum(values, scrap), scrap)
        expect = jnp.einsum(
            "zw,swk->szk", transition, continuation, precision=lax.Precision.HIGHEST
        )
        forward_value = 0.9 * expect - install_cost[None, None, :]

        def by_rows(stacked):
            items, prod_part, cap_whole = stacked.shape
            flattened = stacked.reshape(items * prod_part, cap_whole)
            return best_reply(flattened, 0, cap_whole, 0).reshape(items, prod_part, cap_whole)

        spread_best = exchange_in_groups(forward_value, CAP, 1, 2, by_rows, 0, 0)
        best = lax.all_to_all(spread_best, CAP, split_axis=2, concat_axis=1, tiled=True)
        values = jnp.where(live, relative[:, None, None] * output + best, scrap)
    return (values, relative)


def solution(mesh):
    finer = Mesh(mesh.devices.reshape(mesh.shape["sector"], 4, 4), ("sector", "cap_0", "cap_1"))
    placed = (
        P("sector", None, CAP),
        P("sector", None, CAP),
        P("sector", None, CAP),
        P("sector"),
        P("sector"),
        P(),
        P(CAP),
    )
    return jax.shard_map(
        on_device,
        mesh=finer,
        in_specs=placed,
        out_specs=(P("sector", None, CAP), P("sector")),
        check_vma=False,
    )
```

profile of v0, /device:TPU:1, one launch (start us, length us, event | category | flops | bytes accessed | tf_op | source)
XLA Modules:
  0.0 253.3 jit_solution(15050220878326860343)
XLA Ops:
  1.5 1.3 multiply_reduce_fusion.1
  2.7 9.5 %psum.28 = f32[8]{0:T(128)S(1)} all-reduce(f32[8]{0:T(128)S(1)} %get-tuple-element.342), channel_id=1, replica_groups=mesh['sector'=32,'cap_0'=4,'cap_1'=4] {'cap_0'}, use_global_device_ids=true, to_apply=%region_1.2 | all-reduce | flops 8 | bytes 64 | tf_op jit(solution)/shard_map/psum | solution.py:17
  12.3 8.5 %psum.29 = f32[8]{0:T(128)S(1)} all-reduce(f32[8]{0:T(128)S(1)} %psum.28), channel_id=1, replica_groups=mesh['sector'=32,'cap_0'=4,'cap_1'=4] {'cap_1'}, use_global_device_ids=true, to_apply=%region_2.3 | all-reduce | flops 8 | bytes 64 | tf_op jit(solution)/shard_map/psum | solution.py:17
  20.7 1.3 sqrt_reduce_fusion.1
  22.0 1.3 broadcast_in_dim.162
  23.3 20.0 %all-to-all-start = ((f32[32,1,1]{2,1,0:T(1,128)}), f32[32,1,1]{2,1,0:T(1,128)S(1)}, u32[]{:S(2)}, u32[]{:S(2)}) async-start(f32[32,1,1]{2,1,0:T(1,128)} %broadcast_in_dim.162), calls=%async_computation | async-start | bytes 32768 | tf_op jit(solution)/shard_map/all_to_all | solution.py:22
  43.3 1.2 fusion.21
  45.1 9.9 %all-to-all-done = f32[32,1,1]{2,1,0:T(1,128)S(1)} async-done(((f32[32,1,1]{2,1,0:T(1,128)}), f32[32,1,1]{2,1,0:T(1,128)S(1)}, u32[]{:S(2)}, u32[]{:S(2)}) %all-to-all-start) | async-done | bytes 160 | tf_op jit(solution)/shard_map/all_to_all | solution.py:22
  55.0 3.5 %all-to-all-start.1 = ((f32[4,32,128]{2,0,1:T(4,128)}), f32[4,32,128]{2,0,1:T(4,128)S(1)}, u32[]{:S(2)}, u32[]{:S(2)}) async-start(f32[4,32,128]{2,0,1:T(4,128)} %copy.64), calls=%async_computation.1 | async-start | bytes 131072 | tf_op jit(solution)/shard_map/all_to_all | solution.py:42
  60.9 4.1 %all-to-all-done.1 = f32[4,32,128]{2,0,1:T(4,128)S(1)} async-done(((f32[4,32,128]{2,0,1:T(4,128)}), f32[4,32,128]{2,0,1:T(4,128)S(1)}, u32[]{:S(2)}, u32[]{:S(2)}) %all-to-all-start.1) | async-done | bytes 65568 | tf_op jit(solution)/shard_map/all_to_all | solution.py:42
  65.0 3.5 %all-to-all-start.2 = ((f32[4,32,128]{2,0,1:T(4,128)}), f32[4,32,128]{2,0,1:T(4,128)S(1)}, u32[]{:S(2)}, u32[]{:S(2)}) async-start(f32[4,32,128]{2,0,1:T(4,128)} %copy.67), calls=%async_computation.2 | async-start | bytes 131072 | tf_op jit(solution)/shard_map/all_to_all | solution.py:42
  69.2 19.6 %while.56 = (s32[]{:T(128)}, f32[4,8,512]{2,1,0:T(8,128)S(1)}, f32[4,2,2048]{2,1,0:T(2,128)}, s32[4]{0:T(128)S(1)}, f32[8,2048]{1,0:T(8,128)S(1)}, /*index=5*/s32[]{:T(128)}, s32[1]{0:T(128)}) while((s32[]{:T(128)}, f32[4,8,512]{2,1,0:T(8,128)S(1)}, f32[4,2,2048]{2,1,0:T(2,128)}, s32[4]{0:T(128)S(1)}, f32[8,2048]{1,0:T(8,128)S(1)}, ...), condition=%wide.wide.region_7.8_spmd, body=%wide.wide.region_5.7_spmd.sunk | while | flops 24128516 | bytes 8536181 | solution.py:82
  70.4 1.2 fusion.66
  71.6 2.5 subtract_reduce_fusion.12
  75.3 1.2 fusion.66
  76.5 2.5 subtract_reduce_fusion.12
  80.2 1.2 fusion.66
  81.4 2.5 subtract_reduce_fusion.12
  85.1 1.2 fusion.66
  86.3 2.5 subtract_reduce_fusion.12
  89.7 20.5 %while.57 = (s32[]{:T(128)}, f32[4,8,512]{2,1,0:T(8,128)S(1)}, f32[4,2,2048]{2,1,0:T(2,128)}, s32[4]{0:T(128)S(1)}, f32[8,2048]{1,0:T(8,128)S(1)}, /*index=5*/s32[]{:T(128)}, s32[1]{0:T(128)}) while((s32[]{:T(128)}, f32[4,8,512]{2,1,0:T(8,128)S(1)}, f32[4,2,2048]{2,1,0:T(2,128)}, s32[4]{0:T(128)S(1)}, f32[8,2048]{1,0:T(8,128)S(1)}, ...), condition=%wide.wide.region_10.11_spmd, body=%wide.wide.region_8.10_spmd.sunk | while | flops 24128516 | bytes 8536181 | solution.py:82
  91.1 1.2 fusion.69
  92.3 2.5 subtract_reduce_fusion.13
  96.2 1.2 fusion.69
  97.4 2.5 subtract_reduce_fusion.13
  101.4 1.2 fusion.69
  102.6 2.5 subtract_reduce_fusion.13
  106.5 1.2 fusion.69
  107.7 2.5 subtract_reduce_fusion.13
  110.4 1.0 copy.70
  111.5 4.0 %reshape.589 = f32[16,1,2048]{2,1,0:T(1,128)} reshape(f32[2048,2,8]{2,1,0:T(2,128)S(1)} %bitcast.81) | data formatting | bytes 262144
  115.5 6.6 %all-to-all-start.3 = ((f32[16,1,2048]{2,1,0:T(1,128)}), f32[16,1,2048]{2,1,0:T(1,128)S(1)}, u32[]{:S(2)}, u32[]{:S(2)}) async-start(f32[16,1,2048]{2,1,0:T(1,128)} %reshape.589), calls=%async_computation.3 | async-start | bytes 262144 | tf_op jit(solution)/shard_map/all_to_all | solution.py:122
  122.1 6.8 %all-to-all-done.3 = f32[16,1,2048]{2,1,0:T(1,128)S(1)} async-done(((f32[16,1,2048]{2,1,0:T(1,128)}), f32[16,1,2048]{2,1,0:T(1,128)S(1)}, u32[]{:S(2)}, u32[]{:S(2)}) %all-to-all-start.3) | async-done | bytes 131104 | tf_op jit(solution)/shard_map/all_to_all | solution.py:122
  130.4 3.2 %reshape.590 = f32[2048,2,8]{2,1,0:T(2,128)S(1)} reshape(f32[16,2048]{1,0:T(8,128)S(1)} %reduce.2) | data formatting | bytes 262144
  134.7 6.6 %psum.30 = f32[8]{0:T(128)S(1)} all-reduce(f32[8]{0:T(128)S(1)} %multiply_reduce_fusion), channel_id=1, replica_groups=mesh['sector'=32,'cap_0'=4,'cap_1'=4] {'cap_0'}, use_global_device_ids=true, to_apply=%region_12.13 | all-reduce | flops 8 | bytes 64 | tf_op jit(solution)/shard_map/psum | solution.py:17
  141.6 6.9 %psum.31 = f32[8]{0:T(128)S(1)} all-reduce(f32[8]{0:T(128)S(1)} %psum.30), channel_id=1, replica_groups=mesh['sector'=32,'cap_0'=4,'cap_1'=4] {'cap_1'}, use_global_device_ids=true, to_apply=%region_13.14 | all-reduce | flops 8 | bytes 64 | tf_op jit(solution)/shard_map/psum | solution.py:17
  149.3 1.3 broadcast_in_dim.163
  150.6 11.2 %all-to-all-start.4 = ((f32[32,1,1]{2,1,0:T(1,128)}), f32[32,1,1]{2,1,0:T(1,128)S(1)}, u32[]{:S(2)}, u32[]{:S(2)}) async-start(f32[32,1,1]{2,1,0:T(1,128)} %broadcast_in_dim.163), calls=%async_computation.4 | async-start | bytes 32768 | tf_op jit(solution)/shard_map/all_to_all | solution.py:22
  162.5 11.2 %all-to-all-done.4 = f32[32,1,1]{2,1,0:T(1,128)S(1)} async-done(((f32[32,1,1]{2,1,0:T(1,128)}), f32[32,1,1]{2,1,0:T(1,128)S(1)}, u32[]{:S(2)}, u32[]{:S(2)}) %all-to-all-start.4) | async-done | bytes 160 | tf_op jit(solution)/shard_map/all_to_all | solution.py:22
  173.6 3.5 %all-to-all-start.5 = ((f32[4,32,128]{2,0,1:T(4,128)}), f32[4,32,128]{2,0,1:T(4,128)S(1)}, u32[]{:S(2)}, u32[]{:S(2)}) async-start(f32[4,32,128]{2,0,1:T(4,128)} %copy.73), calls=%async_computation.5 | async-start | bytes 131072 | tf_op jit(solution)/shard_map/all_to_all | solution.py:42
  179.6 4.1 %all-to-all-done.5 = f32[4,32,128]{2,0,1:T(4,128)S(1)} async-done(((f32[4,32,128]{2,0,1:T(4,128)}), f32[4,32,128]{2,0,1:T(4,128)S(1)}, u32[]{:S(2)}, u32[]{:S(2)}) %all-to-all-start.5) | async-done | bytes 65568 | tf_op jit(solution)/shard_map/all_to_all | solution.py:42
  183.7 3.5 %all-to-all-start.6 = ((f32[4,32,128]{2,0,1:T(4,128)}), f32[4,32,128]{2,0,1:T(4,128)S(1)}, u32[]{:S(2)}, u32[]{:S(2)}) async-start(f32[4,32,128]{2,0,1:T(4,128)} %copy.76), calls=%async_computation.6 | async-start | bytes 131072 | tf_op jit(solution)/shard_map/all_to_all | solution.py:42
  187.8 19.6 %while.58 = (s32[]{:T(128)}, f32[4,8,512]{2,1,0:T(8,128)S(1)}, f32[4,2,2048]{2,1,0:T(2,128)}, s32[4]{0:T(128)S(1)}, f32[8,2048]{1,0:T(8,128)S(1)}, /*index=5*/s32[]{:T(128)}, s32[1]{0:T(128)}) while((s32[]{:T(128)}, f32[4,8,512]{2,1,0:T(8,128)S(1)}, f32[4,2,2048]{2,1,0:T(2,128)}, s32[4]{0:T(128)S(1)}, f32[8,2048]{1,0:T(8,128)S(1)}, ...), condition=%wide.wide.region_18.19_spmd, body=%wide.wide.region_16.18_spmd.sunk | while | flops 24128516 | bytes 8536181 | solution.py:82
  189.0 1.2 fusion.72
  190.2 2.5 subtract_reduce_fusion.14
  194.0 1.2 fusion.72
  195.1 2.5 subtract_reduce_fusion.14
  198.9 1.2 fusion.72
  200.1 2.5 subtract_reduce_fusion.14
  203.8 1.2 fusion.72
  205.0 2.5 subtract_reduce_fusion.14
  208.3 20.5 %while.59 = (s32[]{:T(128)}, f32[4,8,512]{2,1,0:T(8,128)S(1)}, f32[4,2,2048]{2,1,0:T(2,128)}, s32[4]{0:T(128)S(1)}, f32[8,2048]{1,0:T(8,128)S(1)}, /*index=5*/s32[]{:T(128)}, s32[1]{0:T(128)}) while((s32[]{:T(128)}, f32[4,8,512]{2,1,0:T(8,128)S(1)}, f32[4,2,2048]{2,1,0:T(2,128)}, s32[4]{0:T(128)S(1)}, f32[8,2048]{1,0:T(8,128)S(1)}, ...), condition=%wide.wide.region_21.22_spmd, body=%wide.wide.region_19.21_spmd.sunk | while | flops 24128516 | bytes 8536181 | solution.py:82
  209.8 1.2 fusion.75
  210.9 2.5 subtract_reduce_fusion.15
  214.9 1.2 fusion.75
  216.1 2.5 subtract_reduce_fusion.15
  220.0 1.2 fusion.75
  221.2 2.5 subtract_reduce_fusion.15
  225.2 1.2 fusion.75
  226.3 2.5 subtract_reduce_fusion.15
  230.1 4.0 %reshape.591 = f32[16,1,2048]{2,1,0:T(1,128)} reshape(f32[2048,2,8]{2,1,0:T(2,128)S(1)} %bitcast.83) | data formatting | bytes 262144
  234.1 6.6 %all-to-all-start.7 = ((f32[16,1,2048]{2,1,0:T(1,128)}), f32[16,1,2048]{2,1,0:T(1,128)S(1)}, u32[]{:S(2)}, u32[]{:S(2)}) async-start(f32[16,1,2048]{2,1,0:T(1,128)} %reshape.591), calls=%async_computation.7 | async-start | bytes 262144 | tf_op jit(solution)/shard_map/all_to_all | solution.py:122
  240.7 6.9 %all-to-all-done.7 = f32[16,1,2048]{2,1,0:T(1,128)S(1)} async-done(((f32[16,1,2048]{2,1,0:T(1,128)}), f32[16,1,2048]{2,1,0:T(1,128)S(1)}, u32[]{:S(2)}, u32[]{:S(2)}) %all-to-all-start.7) | async-done | bytes 131104 | tf_op jit(solution)/shard_map/all_to_all | solution.py:122
  248.5 3.2 %reshape.592 = f32[2048,2,8]{2,1,0:T(2,128)S(1)} reshape(f32[16,2048]{1,0:T(8,128)S(1)} %reduce.3) | data formatting | bytes 262144
  (170 shorter events, 25.7 us)
Async XLA Ops:
  0.6 42.6 %copy-start = (f32[32,32]{1,0:T(8,128)S(1)}, f32[32,32]{1,0:T(8,128)}, u32[]{:S(2)}) copy-start(f32[32,32]{1,0:T(8,128)} %param.20) | copy-start | bytes 12292
  23.3 31.7 %all-to-all-start = ((f32[32,1,1]{2,1,0:T(1,128)}), f32[32,1,1]{2,1,0:T(1,128)S(1)}, u32[]{:S(2)}, u32[]{:S(2)}) async-start(f32[32,1,1]{2,1,0:T(1,128)} %broadcast_in_dim.162), calls=%async_computation | async-start | bytes 32768 | tf_op jit(solution)/shard_map/all_to_all | solution.py:22
  55.0 10.0 %all-to-all-start.1 = ((f32[4,32,128]{2,0,1:T(4,128)}), f32[4,32,128]{2,0,1:T(4,128)S(1)}, u32[]{:S(2)}, u32[]{:S(2)}) async-start(f32[4,32,128]{2,0,1:T(4,128)} %copy.64), calls=%async_computation.1 | async-start | bytes 131072 | tf_op jit(solution)/shard_map/all_to_all | solution.py:42
  65.0 24.0 %all-to-all-start.2 = ((f32[4,32,128]{2,0,1:T(4,128)}), f32[4,32,128]{2,0,1:T(4,128)S(1)}, u32[]{:S(2)}, u32[]{:S(2)}) async-start(f32[4,32,128]{2,0,1:T(4,128)} %copy.67), calls=%async_computation.2 | async-start | bytes 131072 | tf_op jit(solution)/shard_map/all_to_all | solution.py:42
  68.6 0.6 copy-start.3
  89.1 0.6 copy-start.4
  110.4 24.0 %copy-start.1 = (f32[8,32,128]{2,1,0:T(8,128)S(1)}, f32[8,32,128]{2,1,0:T(8,128)}, u32[]{:S(2)}) copy-start(f32[8,32,128]{2,1,0:T(8,128)} %param.16) | copy-start | bytes 393220
  111.4 29.8 %copy-start.6 = (f32[128]{0:T(128)S(1)}, f32[128]{0:T(128)}, u32[]{:S(2)}) copy-start(f32[128]{0:T(128)} %param.21) | copy-start | bytes 1540
  111.5 37.1 %copy-start.7 = (f32[8]{0:T(128)S(1)}, f32[8]{0:T(128)}, u32[]{:S(2)}) copy-start(f32[8]{0:T(128)} %param.19) | copy-start | bytes 100
  115.5 13.4 %all-to-all-start.3 = ((f32[16,1,2048]{2,1,0:T(1,128)}), f32[16,1,2048]{2,1,0:T(1,128)S(1)}, u32[]{:S(2)}, u32[]{:S(2)}) async-start(f32[16,1,2048]{2,1,0:T(1,128)} %reshape.589), calls=%async_computation.3 | async-start | bytes 262144 | tf_op jit(solution)/shard_map/all_to_all | solution.py:122
  150.6 23.1 %all-to-all-start.4 = ((f32[32,1,1]{2,1,0:T(1,128)}), f32[32,1,1]{2,1,0:T(1,128)S(1)}, u32[]{:S(2)}, u32[]{:S(2)}) async-start(f32[32,1,1]{2,1,0:T(1,128)} %broadcast_in_dim.163), calls=%async_computation.4 | async-start | bytes 32768 | tf_op jit(solution)/shard_map/all_to_all | solution.py:22
  173.6 10.0 %all-to-all-start.5 = ((f32[4,32,128]{2,0,1:T(4,128)}), f32[4,32,128]{2,0,1:T(4,128)S(1)}, u32[]{:S(2)}, u32[]{:S(2)}) async-start(f32[4,32,128]{2,0,1:T(4,128)} %copy.73), calls=%async_computation.5 | async-start | bytes 131072 | tf_op jit(solution)/shard_map/all_to_all | solution.py:42
  183.7 24.0 %all-to-all-start.6 = ((f32[4,32,128]{2,0,1:T(4,128)}), f32[4,32,128]{2,0,1:T(4,128)S(1)}, u32[]{:S(2)}, u32[]{:S(2)}) async-start(f32[4,32,128]{2,0,1:T(4,128)} %copy.76), calls=%async_computation.6 | async-start | bytes 131072 | tf_op jit(solution)/shard_map/all_to_all | solution.py:42
  187.2 0.6 copy-start.5
  207.7 0.6 copy-start.2
  234.1 13.5 %all-to-all-start.7 = ((f32[16,1,2048]{2,1,0:T(1,128)}), f32[16,1,2048]{2,1,0:T(1,128)S(1)}, u32[]{:S(2)}, u32[]{:S(2)}) async-start(f32[16,1,2048]{2,1,0:T(1,128)} %reshape.591), calls=%async_computation.7 | async-start | bytes 262144 | tf_op jit(solution)/shard_map/all_to_all | solution.py:122
  240.7 12.6 %copy-start.8 = (f32[8]{0:T(128)}, f32[8]{0:T(128)S(1)}, u32[]{:S(2)}) copy-start(f32[8]{0:T(128)S(1)} %broadcast_divide_fusion) | copy-start | bytes 100
where the time goes:
time: 256 us; the launch traced here: 253 us
  other arithmetic  67.8 us (26%)
  starting transfers between devices  58.4 us (23%)
  waiting for transfers between devices  42.9 us (17%)
  local copies, waits for them, and re-layouts  36.9 us (14%)
  blocking collectives  31.5 us (12%)
  loops' own time  10.9 us (4%)
  between operations  3.44 us (1%)
    reduce_max x16, other arithmetic, row_step(): return jnp.maximum(empty, jnp.max(group[:, None, :] - charge[None], axis=2))  40 us
    psum x4, blocking collectives, over_axes(): return functools.reduce(lax.psum, axes, x)  31.5 us
    all_to_all x2, starting transfers between devices, from_everyone(): return lax.all_to_all(copies, axis, split_axis=0, concat_axis=0, tiled=True)  31.2 us
    all_to_all x2, waiting for transfers between devices, from_everyone(): return lax.all_to_all(copies, axis, split_axis=0, concat_axis=0, tiled=True)  21 us
    add x16, other arithmetic, charge_of(): return invest + invest * invest / cap_now + fixed  18.9 us
    unnamed x22, local copies, waits for them, and re-layouts  16.5 us
    all_to_all x4, starting transfers between devices, exchange_in_groups(): lax.all_to_all(group, axis, split_axis=split_dim, concat_axis=concat_dim,...  14 us
    all_to_all x2, waiting for transfers between devices, on_device(): lax.all_to_all(spread_best, CAP, split_axis=2, concat_axis=1, tiled=True)  13.7 us
  transfers between devices with their start and end apart: 8, of which 6 were waited for; matrix products, arithmetic and copies ran while one was open for 16% of the time, Pallas kernels for 0%

commit v1 on v0

v1 whole, which is shorter than its diff:
```python
import math

import jax
import jax.numpy as jnp
import numpy as np
from jax import lax
from jax.experimental import pallas as pl
from jax.experimental.pallas import tpu as pltpu
from jax.sharding import PartitionSpec as P

K = 2048
Z = 32
SWEEPS = 2
SEC = 8
CAPS = 16
ZS = 16
ROWS = 16
CHUNK = 32
CHUNKS = K // CHUNK
STEPS = CHUNKS + CAPS - 1
GROUPS = K // 8
LINES = GROUPS + 8 * (CAPS - 1)
SHIFT = 8 * (CAPS - 1)
ENDS = 96
NEG = -1e30
LOG10 = float(np.log(np.float32(10.0)))


def capital_of(positions):
    return 0.2 * jnp.exp(LOG10 * positions.astype(jnp.float32) / (K - 1))


def iota(shape, axis):
    return lax.broadcasted_iota(jnp.int32, shape, axis)


def kernel(
    exit_ref, demand_ref, start_ref, mass_ref, survive_ref, trans_ref, install_ref,
    value_ref, rel_ref,
    forward, heard, heights, lines, table, jumps, table_s, jumps_s,
    reached, folded, reply, best, part, parts, root, pair, both, roots,
    fwd_send, fwd_recv, rep_send, rep_recv, par_send, par_recv, pair_send, pair_recv,
    root_send, root_recv, table_sem,
):
    me = lax.axis_index("cap")
    sec = lax.axis_index("sector")
    core = lax.rem(sec, 2)
    level = sec // 2
    partner = sec + 1 - 2 * core

    def cap_at(d):
        return {"cap": lax.rem(me + d, CAPS)}

    def level_at(d):
        return {"sector": 2 * lax.rem(level + d, ZS) + core}

    barrier = pltpu.get_barrier_semaphore()

    def greet(d, c):
        pl.semaphore_signal(barrier, inc=1, device_id=cap_at(d))
        pl.semaphore_signal(barrier, inc=1, device_id=level_at(d))
        return c

    lax.fori_loop(1, CAPS, greet, 0)
    pl.semaphore_signal(barrier, inc=1, device_id={"sector": partner})

    capital_all = capital_of(iota((CAPS, 128), 0) * 128 + iota((CAPS, 128), 1))
    half = 0.8 * capital_all
    square_all = capital_all * capital_all
    low = iota((8, 128), 1) % 8
    own_place = 2 * low - 8 * (iota((8, 128), 1) // 8) - iota((8, 128), 0)

    def fill(i, c):
        lines[i] = capital_of(16 * (i - SHIFT) + own_place)
        return c

    lax.fori_loop(0, LINES, fill, 0, unroll=8)
    place = me * 128 + iota((1, 128), 1)
    capital = capital_of(place)
    scrap = 0.3 * capital
    log_cap = math.log(0.2) + LOG10 * place.astype(jnp.float32) / (K - 1)
    log_prod = -0.5 + iota((Z, 128), 0).astype(jnp.float32) / (Z - 1)
    output = jnp.exp(log_prod + 0.6 * log_cap)
    install = install_ref[...]
    lane = iota((ROWS, 128), 1)
    lane_f = lane.astype(jnp.float32)

    def fwd_copy(sweep, d):
        peer = lax.rem(me + d, CAPS)
        return pltpu.make_async_remote_copy(
            forward.at[sweep, peer], heard.at[sweep, me], fwd_send.at[sweep, d], fwd_recv.at[sweep, d],
            device_id=cap_at(d))

    def rep_copy(sweep, d):
        peer = lax.rem(me + d, CAPS)
        return pltpu.make_async_remote_copy(
            reply.at[sweep, peer], best.at[sweep, me], rep_send.at[sweep, d], rep_recv.at[sweep, d],
            device_id=cap_at(d))

    def par_copy(sweep, d):
        return pltpu.make_async_remote_copy(
            part.at[sweep], parts.at[sweep, me], par_send.at[sweep, d], par_recv.at[sweep, d],
            device_id=cap_at(d))

    def root_copy(sweep, d):
        return pltpu.make_async_remote_copy(
            both.at[sweep], roots.at[sweep, level], root_send.at[sweep, d], root_recv.at[sweep, d],
            device_id=level_at(d))

    def start_all(copy, sweep):
        def one(d, c):
            copy(sweep, d).start()
            return c
        lax.fori_loop(1, CAPS, one, 0)

    def wait_all(copy, sweep):
        def one(d, c):
            copy(sweep, d).wait()
            return c
        lax.fori_loop(1, CAPS, one, 0)

    value_ref[...] = start_ref[...]

    def sweep_body(sweep, carry):
        sums = []
        for s in range(SEC):
            live = (survive_ref[s] == 1) & (iota((Z, 128), 0) >= exit_ref[s])
            values = value_ref[s]
            staying = jnp.where(live, jax.nn.sigmoid((values - scrap) * 2.0), 0.0)
            sums.append(jnp.sum(mass_ref[s] * staying * output, axis=0, keepdims=True))
            continuation = jnp.where(live, jnp.maximum(values, scrap), scrap)
            expect = lax.dot_general(
                trans_ref[...], continuation, (((1,), (0,)), ((), ())),
                precision=lax.Precision.HIGHEST, preferred_element_type=jnp.float32)
            ahead = 0.9 * expect - install
            forward[sweep, 2 * s] = ahead[:ROWS]
            forward[sweep, 2 * s + 1] = ahead[ROWS:]
        part[sweep] = jnp.concatenate(sums, axis=0)

        @pl.when(sweep == 0)
        def _():
            pl.semaphore_wait(barrier, CAPS - 1 + ZS - 1 + 1)

        start_all(par_copy, sweep)
        start_all(fwd_copy, sweep)
        heard[sweep, me] = forward[sweep, me]
        parts[sweep, me] = part[sweep]
        wait_all(par_copy, sweep)
        whole = jnp.sum(jnp.sum(parts[sweep], axis=0), axis=1, keepdims=True)
        supply = 1.0 + jnp.broadcast_to(whole, (SEC, 128)) / (Z * K)
        demand = jnp.zeros((SEC, 128), jnp.float32)
        for s in range(SEC):
            demand = jnp.where(iota((SEC, 128), 0) == s, demand_ref[s], demand)
        prices = jnp.sqrt(demand / supply)
        root[sweep] = jnp.sum(jnp.sqrt(prices), axis=0, keepdims=True)
        to_pair = pltpu.make_async_remote_copy(
            root.at[sweep], pair.at[sweep], pair_send.at[sweep], pair_recv.at[sweep],
            device_id={"sector": partner})
        to_pair.start()
        to_pair.wait()
        both[sweep] = root[sweep] + pair[sweep]
        start_all(root_copy, sweep)
        roots[sweep, level] = both[sweep]

        wait_all(fwd_copy, sweep)

        def spread(i, c):
            rows = [heard[sweep, i] + 0.8 * capital_of(i * 128 + iota((1, 128), 1))]
            for bit in (64, 32, 16, 8):
                high = (lane // bit) % 2 == 1
                wide = []
                for x in rows:
                    turned = pltpu.roll(x, bit, 1)
                    wide += [jnp.where(high, turned, x), jnp.where(high, x, turned)]
                rows = wide
            for g in range(16):
                heights[16 * i + g] = rows[g]
            return c

        lax.fori_loop(0, CAPS, spread, 0)

        tall = heard[sweep] + half[:, None, :]
        source = lax.broadcasted_iota(jnp.int32, (CAPS, ROWS, 128), 0).astype(jnp.float32)
        chunks = []
        for b in range(1, CAPS):
            rate = 1.0 / (0.2 * math.exp(LOG10 * 128 * b / (K - 1)))
            here = tall - (square_all * rate)[:, None, :]
            top = jnp.max(here, axis=0)
            where = jnp.min(jnp.where(here == top[None], source, 1e9), axis=0)
            peak = jnp.max(top, axis=1, keepdims=True)
            spot = where * (128 // CHUNK) + (lane // CHUNK).astype(jnp.float32)
            chunk = jnp.min(jnp.where(top == peak, spot, 1e9), axis=1, keepdims=True)
            chunk = jnp.broadcast_to(chunk, (ROWS, 128))
            chunks.append(jnp.maximum(chunk, chunks[-1]) if chunks else chunk)
        chunks.append(jnp.full((ROWS, 128), float(CHUNKS - 1), jnp.float32))
        block = jnp.zeros((ROWS, 128), jnp.float32)
        jump = jnp.zeros((ROWS, 128), jnp.float32)
        for b in range(1, CAPS):
            first = chunks[b - 1] + float(b)
            block = block + jnp.where(first <= lane_f, 1.0, 0.0)
            jump = jnp.where(first == lane_f, NEG, jump)
        group = 4.0 * (lane_f - block)
        line = group - 8.0 * block + float(SHIFT)
        for b in range(CAPS):
            group = jnp.where(lane == ENDS + b, chunks[b] + float(b), group)
        table[:ROWS] = jnp.clip(group.astype(jnp.int32), 0, jnp.where(lane < ENDS, GROUPS - 4, STEPS - 1))
        table[ROWS:] = jnp.clip(line.astype(jnp.int32), 0, LINES - 4)
        jumps[...] = jump
        to_table = pltpu.make_async_copy(table, table_s, table_sem.at[0])
        to_jumps = pltpu.make_async_copy(jumps, jumps_s, table_sem.at[1])
        to_table.start()
        to_jumps.start()
        to_table.wait()
        to_jumps.wait()

        def step(t, accs):
            out = []
            for r in range(ROWS):
                at_height = jnp.clip(table_s[r, t], 0, GROUPS - 4)
                at_line = jnp.clip(table_s[ROWS + r, t], 0, LINES - 4)
                value = heights[pl.ds(at_height, 4), r:r + 1, :] - lines[pl.ds(at_line, 4)]
                acc = jnp.maximum(jnp.max(value, axis=0), accs[r] + jumps_s[r, t])
                reached[r, t] = acc
                out.append(acc)
            return tuple(out)

        lax.fori_loop(0, STEPS, step, tuple(jnp.full((8, 128), NEG, jnp.float32) for _ in range(ROWS)))

        for h in range(2):
            odd = iota((ROWS * 8, 128), 1)
            tops = []
            for p in range(8):
                tops.append(jnp.concatenate(
                    [reached[r, jnp.clip(table_s[r, ENDS + 8 * h + p], 0, STEPS - 1)] for r in range(ROWS)], axis=0))
            for bit in (4, 2, 1):
                high = (odd // bit) % 2 == 1
                less = []
                for i in range(len(tops) // 2):
                    x, y = tops[i], tops[i + len(tops) // 2]
                    mine = jnp.where(high, y, x)
                    other = jnp.where(high, x, y)
                    other = jnp.where(high, pltpu.roll(other, bit, 1), pltpu.roll(other, 128 - bit, 1))
                    less.append(jnp.maximum(mine, other))
                tops = less
            folded[h] = tops[0].reshape(ROWS, 8, 128)
            ways = [folded[h, :, q, :] for q in range(8)]
            for bit in (4, 2, 1):
                high = (lane // bit) % 2 == 1
                for q in range(8):
                    if q & bit == 0:
                        x, y = ways[q], ways[q + bit]
                        ways[q] = jnp.where(high, pltpu.roll(y, bit, 1), x)
                        ways[q + bit] = jnp.where(high, y, pltpu.roll(x, 128 - bit, 1))
            for p in range(8):
                reply[sweep, 8 * h + p] = ways[p]
        start_all(rep_copy, sweep)
        best[sweep, me] = reply[sweep, me]
        wait_all(root_copy, sweep)
        root_sum = jnp.sum(roots[sweep], axis=0)
        price_index = root_sum / (SEC * 2 * ZS)
        price_index = price_index * price_index
        relative = prices / price_index
        wait_all(rep_copy, sweep)
        for s in range(SEC):
            for h in range(2):
                top = best[sweep, 2 * s + h] - 1.41 * capital
                stay = forward[sweep, 2 * s + h] - 0.11 * capital
                gain = jnp.maximum(top, stay)
                rows = slice(h * ROWS, (h + 1) * ROWS)
                live = (survive_ref[s, rows] == 1) & (iota((ROWS, 128), 0) + h * ROWS >= exit_ref[s])
                value_ref[s, rows] = jnp.where(live, relative[s:s + 1] * output[rows] + gain, scrap)
        flat = jnp.where(iota((SEC, 128), 0) == iota((SEC, 128), 1), relative, 0.0)
        rel_ref[...] = jnp.sum(flat, axis=0, keepdims=True)[:, :SEC]
        return carry

    lax.fori_loop(0, SWEEPS, sweep_body, 0)


def on_device(start_value, firm_mass, survive, exit_index, demand, transition, install_cost):
    f32 = jnp.float32
    vmem = pl.BlockSpec(memory_space=pltpu.VMEM)
    smem = pl.BlockSpec(memory_space=pltpu.SMEM)
    dma = pltpu.SemaphoreType.DMA
    values, relative = pl.pallas_call(
        kernel,
        out_shape=(jax.ShapeDtypeStruct((SEC, Z, 128), f32), jax.ShapeDtypeStruct((1, SEC), f32)),
        in_specs=[smem, smem, vmem, vmem, vmem, vmem, vmem],
        out_specs=(vmem, vmem),
        scratch_shapes=[
            pltpu.VMEM((SWEEPS, CAPS, ROWS, 128), f32),
            pltpu.VMEM((SWEEPS, CAPS, ROWS, 128), f32),
            pltpu.VMEM((GROUPS, ROWS, 128), f32),
            pltpu.VMEM((LINES, 8, 128), f32),
            pltpu.VMEM((2 * ROWS, 128), jnp.int32),
            pltpu.VMEM((ROWS, 128), f32),
            pltpu.SMEM((2 * ROWS, 128), jnp.int32),
            pltpu.SMEM((ROWS, 128), f32),
            pltpu.VMEM((ROWS, STEPS, 8, 128), f32),
            pltpu.VMEM((2, ROWS, 8, 128), f32),
            pltpu.VMEM((SWEEPS, CAPS, ROWS, 128), f32),
            pltpu.VMEM((SWEEPS, CAPS, ROWS, 128), f32),
            pltpu.VMEM((SWEEPS, SEC, 128), f32),
            pltpu.VMEM((SWEEPS, CAPS, SEC, 128), f32),
            pltpu.VMEM((SWEEPS, 1, 128), f32),
            pltpu.VMEM((SWEEPS, 1, 128), f32),
            pltpu.VMEM((SWEEPS, 1, 128), f32),
            pltpu.VMEM((SWEEPS, ZS, 1, 128), f32),
            dma((SWEEPS, CAPS)), dma((SWEEPS, CAPS)), dma((SWEEPS, CAPS)), dma((SWEEPS, CAPS)),
            dma((SWEEPS, CAPS)), dma((SWEEPS, CAPS)), dma((SWEEPS,)), dma((SWEEPS,)),
            dma((SWEEPS, ZS)), dma((SWEEPS, ZS)), dma((2,)),
        ],
        compiler_params=pltpu.CompilerParams(
            collective_id=0, has_side_effects=True, vmem_limit_bytes=40 << 20),
    )(exit_index, demand, start_value, firm_mass, survive, transition, install_cost.reshape(1, 128))
    return values, relative.reshape(SEC)


def solution(mesh):
    placed = (
        P("sector", None, "cap"),
        P("sector", None, "cap"),
        P("sector", None, "cap"),
        P("sector"),
        P("sector"),
        P(),
        P("cap"),
    )
    return jax.shard_map(
        on_device,
        mesh=mesh,
        in_specs=placed,
        out_specs=(P("sector", None, "cap"), P("sector")),
        check_vma=False,
    )
```

time: 256 us -> 78.3 us (0.31)
  Pallas kernels: 0 us -> 72.1 us
  other arithmetic: 67.8 us -> 0 us
  starting transfers between devices: 58.4 us -> 0 us
  waiting for transfers between devices: 42.9 us -> 0 us
  local copies, waits for them, and re-layouts: 36.9 us -> 5.26 us
  blocking collectives: 31.5 us -> 0 us
  loops' own time: 10.9 us -> 0 us
  between operations: 3.44 us -> 0.67 us
    pallas_call x0 -> x1, Pallas kernels: none -> 72.1 us  [on_device(): pl.pallas_call(kernel, out_shape=(jax.ShapeDtypeStruct((SEC, Z, 128), f32...]
    all_to_all x8 -> x0, starting transfers between devices: 58.4 us -> none  [the longest x2 31.2 us: from_everyone(): return lax.all_to_all(copies, axis, split_axis=0, concat_axis=0, tiled=True)]
    all_to_all x8 -> x0, waiting for transfers between devices: 42.9 us -> none  [the longest x2 21 us: from_everyone(): return lax.all_to_all(copies, axis, split_axis=0, concat_axis=0, tiled=True)]
    reduce_max x16 -> x0, other arithmetic: 40 us -> none  [row_step(): return jnp.maximum(empty, jnp.max(group[:, None, :] - charge[None], axis=2))]
    psum x4 -> x0, blocking collectives: 31.5 us -> none  [over_axes(): return functools.reduce(lax.psum, axes, x)]
    add x32 -> x0, other arithmetic: 18.9 us -> none  [the longest x16 18.9 us: charge_of(): return invest + invest * invest / cap_now + fixed]
    unnamed x22 -> x16, local copies, waits for them, and re-layouts: 16.5 us -> 5.26 us
    another operation x4 -> x0, loops' own time: 10.9 us -> none  [one_group(): pieces = lax.map(row_step, jnp.arange(row_steps, dtype=jnp.int32))]
  transfers between devices with their start and end apart: 8 -> 0, of which waited for: 6 -> 0; matrix products, arithmetic and copies ran while one was open for 16% -> 0% of each run, Pallas kernels for 0% -> 0%
where the time goes in v1:
time: 78.3 us; the launch traced here: 78 us
  Pallas kernels  72.1 us (92%)
  local copies, waits for them, and re-layouts  5.26 us (7%)
    pallas_call x1, Pallas kernels, on_device(): pl.pallas_call(kernel, out_shape=(jax.ShapeDtypeStruct((SEC, Z, 128), f32...  72.1 us
    unnamed x16, local copies, waits for them, and re-layouts  5.26 us

profile of v1, /device:TPU:1, one launch (start us, length us, event | category | flops | bytes accessed | tf_op | source)
XLA Modules:
  0.0 78.0 jit_solution(12382516376038368477)
XLA Ops:
  0.6 0.0 copy-start.6
  0.6 0.0 copy-start.5
  0.7 0.0 copy-start.4
  0.7 0.6 copy-done.6
  1.3 0.0 copy-done.5
  1.3 0.0 copy-done.4
  1.3 0.0 copy-start
  1.3 0.9 %copy-done = f32[8,32,128]{2,1,0:T(8,128)S(1)} copy-done((f32[8,32,128]{2,1,0:T(8,128)S(1)}, f32[8,32,128]{2,1,0:T(8,128)}, u32[]{:S(2)}) %copy-start) | copy-done | bytes 131096
  2.2 0.0 copy-start.1
  2.2 0.9 %copy-done.1 = f32[8,32,128]{2,1,0:T(8,128)S(1)} copy-done((f32[8,32,128]{2,1,0:T(8,128)S(1)}, f32[8,32,128]{2,1,0:T(8,128)}, u32[]{:S(2)}) %copy-start.1) | copy-done | bytes 131096
  3.1 0.0 copy-start.2
  3.1 0.9 %copy-done.2 = s32[8,32,128]{2,1,0:T(8,128)S(1)} copy-done((s32[8,32,128]{2,1,0:T(8,128)S(1)}, s32[8,32,128]{2,1,0:T(8,128)}, u32[]{:S(2)}) %copy-start.2) | copy-done | bytes 131096
  4.0 0.0 copy-start.3
  4.0 0.7 copy-done.3
  4.8 72.1 %shard_map.86 = (f32[8,32,128]{2,1,0:T(8,128)S(1)}, f32[1,8]{1,0:T(1,128)S(1)}) custom-call(s32[8]{0:T(128)S(1)} %copy-done.4, f32[8]{0:T(128)S(1)} %copy-done.5, f32[8,32,128]{2,1,0:T(8,128)S(1)} %copy-done, f32[8,32,128]{2,1,0:T(8,128)S(1)} %copy-done.1, s32[8,32,128]{2,1,0:T(8,128)S(1)} %copy-done.2, f32[32,32]{1,0:T(8,128)S(1)} %copy-done.3, ...), custom_call_target="tpu_custom_call" | custom-call | tf_op jit(solution)/shard_map/pallas_call | solution.py:284
  76.9 0.7 copy.11
  77.5 0.5 copy.12
Async XLA Ops:
  0.6 0.7 copy-start.6
  0.6 0.7 copy-start.5
  0.7 0.7 copy-start.4
  1.3 0.9 %copy-start = (f32[8,32,128]{2,1,0:T(8,128)S(1)}, f32[8,32,128]{2,1,0:T(8,128)}, u32[]{:S(2)}) copy-start(f32[8,32,128]{2,1,0:T(8,128)} %start_ref.1) | copy-start | bytes 393220
  2.2 0.9 %copy-start.1 = (f32[8,32,128]{2,1,0:T(8,128)S(1)}, f32[8,32,128]{2,1,0:T(8,128)}, u32[]{:S(2)}) copy-start(f32[8,32,128]{2,1,0:T(8,128)} %mass_ref.1) | copy-start | bytes 393220
  3.1 0.9 %copy-start.2 = (s32[8,32,128]{2,1,0:T(8,128)S(1)}, s32[8,32,128]{2,1,0:T(8,128)}, u32[]{:S(2)}) copy-start(s32[8,32,128]{2,1,0:T(8,128)} %survive_ref.1) | copy-start | bytes 393220
  4.0 0.7 copy-start.3

commit v2 on v1

--- a/solution.py
+++ b/solution.py
@@ -13,11 +13,13 @@
 SWEEPS = 2
 SEC = 8
 CAPS = 16
+REACH = 4
 ZS = 16
 ROWS = 16
 CHUNK = 32
 CHUNKS = K // CHUNK
 STEPS = CHUNKS + CAPS - 1
+SPLIT = 53
 GROUPS = K // 8
 LINES = GROUPS + 8 * (CAPS - 1)
 SHIFT = 8 * (CAPS - 1)
@@ -35,12 +37,13 @@
 
 
 def kernel(
-    exit_ref, demand_ref, start_ref, mass_ref, survive_ref, trans_ref, install_ref,
+    exit_ref, demand_ref, start_hbm, mass_hbm, survive_hbm, trans_hbm, install_hbm,
     value_ref, rel_ref,
     forward, heard, heights, lines, table, jumps, table_s, jumps_s,
-    reached, folded, reply, best, part, parts, root, pair, both, roots,
+    reached, folded, reply, best, part, parts, root, pair, both, near, quad, far,
+    mass_ref, survive_ref, trans_ref, install_ref,
     fwd_send, fwd_recv, rep_send, rep_recv, par_send, par_recv, pair_send, pair_recv,
-    root_send, root_recv, table_sem,
+    near_send, near_recv, far_send, far_recv, table_sem, load_sem,
 ):
     me = lax.axis_index("cap")
     sec = lax.axis_index("sector")
@@ -52,16 +55,26 @@
         return {"cap": lax.rem(me + d, CAPS)}
 
     def level_at(d):
-        return {"sector": 2 * lax.rem(level + d, ZS) + core}
+        return {"sector": 2 * lax.rem(level + d + ZS, ZS) + core}
 
     barrier = pltpu.get_barrier_semaphore()
 
     def greet(d, c):
         pl.semaphore_signal(barrier, inc=1, device_id=cap_at(d))
+        return c
+
+    loads = [
+        pltpu.make_async_copy(source, target, load_sem.at[i])
+        for i, (source, target) in enumerate((
+            (start_hbm, value_ref), (mass_hbm, mass_ref), (survive_hbm, survive_ref),
+            (trans_hbm, trans_ref), (install_hbm, install_ref)))
+    ]
+    for load in loads:
+        load.start()
+    lax.fori_loop(1, CAPS, greet, 0)
+    for d in range(1, REACH + 1):
         pl.semaphore_signal(barrier, inc=1, device_id=level_at(d))
-        return c
-
-    lax.fori_loop(1, CAPS, greet, 0)
+        pl.semaphore_signal(barrier, inc=1, device_id=level_at(-d))
     pl.semaphore_signal(barrier, inc=1, device_id={"sector": partner})
 
     capital_all = capital_of(iota((CAPS, 128), 0) * 128 + iota((CAPS, 128), 1))
@@ -81,7 +94,6 @@
     log_cap = math.log(0.2) + LOG10 * place.astype(jnp.float32) / (K - 1)
     log_prod = -0.5 + iota((Z, 128), 0).astype(jnp.float32) / (Z - 1)
     output = jnp.exp(log_prod + 0.6 * log_cap)
-    install = install_ref[...]
     lane = iota((ROWS, 128), 1)
     lane_f = lane.astype(jnp.float32)
 
@@ -102,10 +114,16 @@
             part.at[sweep], parts.at[sweep, me], par_send.at[sweep, d], par_recv.at[sweep, d],
             device_id=cap_at(d))
 
-    def root_copy(sweep, d):
-        return pltpu.make_async_remote_copy(
-            both.at[sweep], roots.at[sweep, level], root_send.at[sweep, d], root_recv.at[sweep, d],
-            device_id=level_at(d))
+    def near_copy(sweep, d):
+        return pltpu.make_async_remote_copy(
+            both.at[sweep], near.at[sweep, d], near_send.at[sweep, d], near_recv.at[sweep, d],
+            device_id=level_at(-d))
+
+    def far_copy(sweep, i):
+        return pltpu.make_async_remote_copy(
+            far.at[sweep, 1] if i == 2 else quad.at[sweep], far.at[sweep, i],
+            far_send.at[sweep, i], far_recv.at[sweep, i],
+            device_id=level_at(REACH if i == 0 else -REACH))
 
     def start_all(copy, sweep):
         def one(d, c):
@@ -119,7 +137,9 @@
             return c
         lax.fori_loop(1, CAPS, one, 0)
 
-    value_ref[...] = start_ref[...]
+    for load in loads:
+        load.wait()
+    install = install_ref[...]
 
     def sweep_body(sweep, carry):
         sums = []
@@ -139,7 +159,7 @@
 
         @pl.when(sweep == 0)
         def _():
-            pl.semaphore_wait(barrier, CAPS - 1 + ZS - 1 + 1)
+            pl.semaphore_wait(barrier, CAPS - 1 + 2 * REACH + 1)
 
         start_all(par_copy, sweep)
         start_all(fwd_copy, sweep)
@@ -157,12 +177,12 @@
             root.at[sweep], pair.at[sweep], pair_send.at[sweep], pair_recv.at[sweep],
             device_id={"sector": partner})
         to_pair.start()
+
+        wait_all(fwd_copy, sweep)
         to_pair.wait()
         both[sweep] = root[sweep] + pair[sweep]
-        start_all(root_copy, sweep)
-        roots[sweep, level] = both[sweep]
-
-        wait_all(fwd_copy, sweep)
+        for d in range(1, REACH):
+            near_copy(sweep, d).start()
 
         def spread(i, c):
             rows = [heard[sweep, i] + 0.8 * capital_of(i * 128 + iota((1, 128), 1))]
@@ -216,22 +236,30 @@
         def step(t, accs):
             out = []
             for r in range(ROWS):
-                at_height = jnp.clip(table_s[r, t], 0, GROUPS - 4)
-                at_line = jnp.clip(table_s[ROWS + r, t], 0, LINES - 4)
+                at_height = table_s[r, t]
+                at_line = table_s[ROWS + r, t]
                 value = heights[pl.ds(at_height, 4), r:r + 1, :] - lines[pl.ds(at_line, 4)]
                 acc = jnp.maximum(jnp.max(value, axis=0), accs[r] + jumps_s[r, t])
                 reached[r, t] = acc
                 out.append(acc)
             return tuple(out)
 
-        lax.fori_loop(0, STEPS, step, tuple(jnp.full((8, 128), NEG, jnp.float32) for _ in range(ROWS)))
+        accs = lax.fori_loop(0, SPLIT, step, tuple(jnp.full((8, 128), NEG, jnp.float32) for _ in range(ROWS)))
+        four = both[sweep]
+        for d in range(1, REACH):
+            near_copy(sweep, d).wait()
+            four = four + near[sweep, d]
+        quad[sweep] = four
+        far_copy(sweep, 0).start()
+        far_copy(sweep, 1).start()
+        lax.fori_loop(SPLIT, STEPS, step, accs)
 
         for h in range(2):
             odd = iota((ROWS * 8, 128), 1)
             tops = []
             for p in range(8):
                 tops.append(jnp.concatenate(
-                    [reached[r, jnp.clip(table_s[r, ENDS + 8 * h + p], 0, STEPS - 1)] for r in range(ROWS)], axis=0))
+                    [reached[r, table_s[r, ENDS + 8 * h + p]] for r in range(ROWS)], axis=0))
             for bit in (4, 2, 1):
                 high = (odd // bit) % 2 == 1
                 less = []
@@ -255,8 +283,11 @@
                 reply[sweep, 8 * h + p] = ways[p]
         start_all(rep_copy, sweep)
         best[sweep, me] = reply[sweep, me]
-        wait_all(root_copy, sweep)
-        root_sum = jnp.sum(roots[sweep], axis=0)
+        far_copy(sweep, 1).wait()
+        far_copy(sweep, 2).start()
+        far_copy(sweep, 0).wait()
+        far_copy(sweep, 2).wait()
+        root_sum = quad[sweep] + far[sweep, 0] + far[sweep, 1] + far[sweep, 2]
         price_index = root_sum / (SEC * 2 * ZS)
         price_index = price_index * price_index
         relative = prices / price_index
@@ -284,7 +315,7 @@
     values, relative = pl.pallas_call(
         kernel,
         out_shape=(jax.ShapeDtypeStruct((SEC, Z, 128), f32), jax.ShapeDtypeStruct((1, SEC), f32)),
-        in_specs=[smem, smem, vmem, vmem, vmem, vmem, vmem],
+        in_specs=[smem, smem] + [pl.BlockSpec(memory_space=pl.ANY)] * 5,
         out_specs=(vmem, vmem),
         scratch_shapes=[
             pltpu.VMEM((SWEEPS, CAPS, ROWS, 128), f32),
@@ -304,13 +335,19 @@
             pltpu.VMEM((SWEEPS, 1, 128), f32),
             pltpu.VMEM((SWEEPS, 1, 128), f32),
             pltpu.VMEM((SWEEPS, 1, 128), f32),
-            pltpu.VMEM((SWEEPS, ZS, 1, 128), f32),
+            pltpu.VMEM((SWEEPS, REACH, 1, 128), f32),
+            pltpu.VMEM((SWEEPS, 1, 128), f32),
+            pltpu.VMEM((SWEEPS, 3, 1, 128), f32),
+            pltpu.VMEM((SEC, Z, 128), f32),
+            pltpu.VMEM((SEC, Z, 128), jnp.int32),
+            pltpu.VMEM((Z, Z), f32),
+            pltpu.VMEM((1, 128), f32),
             dma((SWEEPS, CAPS)), dma((SWEEPS, CAPS)), dma((SWEEPS, CAPS)), dma((SWEEPS, CAPS)),
             dma((SWEEPS, CAPS)), dma((SWEEPS, CAPS)), dma((SWEEPS,)), dma((SWEEPS,)),
-            dma((SWEEPS, ZS)), dma((SWEEPS, ZS)), dma((2,)),
+            dma((SWEEPS, REACH)), dma((SWEEPS, REACH)), dma((SWEEPS, 3)), dma((SWEEPS, 3)), dma((2,)), dma((5,)),
         ],
         compiler_params=pltpu.CompilerParams(
-            collective_id=0, has_side_effects=True, vmem_limit_bytes=40 << 20),
+            collective_id=0, has_side_effects=True, vmem_limit_bytes=60 << 20),
     )(exit_index, demand, start_value, firm_mass, survive, transition, install_cost.reshape(1, 128))
     return values, relative.reshape(SEC)
 

time: 78.3 us -> 68.6 us (0.88)
  Pallas kernels: 72.1 us -> 65.7 us
  local copies, waits for them, and re-layouts: 5.26 us -> 2.08 us
    pallas_call x1, Pallas kernels: 72.1 us -> 65.7 us  [on_device(): pl.pallas_call(kernel, out_shape=(jax.ShapeDtypeStruct((SEC, Z, 128), f32...]
    unnamed x16 -> x4, local copies, waits for them, and re-layouts: 5.26 us -> 2.08 us
where the time goes in v2:
time: 68.6 us; the launch traced here: 68.5 us
  Pallas kernels  65.7 us (96%)
  local copies, waits for them, and re-layouts  2.08 us (3%)
    pallas_call x1, Pallas kernels, on_device(): pl.pallas_call(kernel, out_shape=(jax.ShapeDtypeStruct((SEC, Z, 128), f32...  65.7 us
    unnamed x4, local copies, waits for them, and re-layouts  2.08 us

profile of v2, /device:TPU:1, one launch (start us, length us, event | category | flops | bytes accessed | tf_op | source)
XLA Modules:
  0.0 68.5 jit_solution(4755497674964980112)
XLA Ops:
  0.6 65.7 %shard_map.86 = (f32[8,32,128]{2,1,0:T(8,128)}, f32[1,8]{1,0:T(1,128)}) custom-call(s32[8]{0:T(128)} %exit_ref.1, f32[8]{0:T(128)} %demand_ref.1, f32[8,32,128]{2,1,0:T(8,128)} %start_hbm.1, f32[8,32,128]{2,1,0:T(8,128)} %mass_hbm.1, s32[8,32,128]{2,1,0:T(8,128)} %survive_hbm.1, f32[32,32]{1,0:T(8,128)} %trans_hbm.1, f32[1,128]{1,0:T(1,128)} %bitcast.2), custom_call_target="tpu_custom_call" | custom-call | tf_op jit(solution)/shard_map/pallas_call | solution.py:315
  66.4 0.0 copy-start
  66.4 1.6 %copy.11 = f32[8,32,128]{2,1,0:T(8,128)} copy(f32[8,32,128]{2,1,0:T(8,128)} %get-tuple-element.8) | data formatting | bytes 262144
  68.0 0.0 copy-done
  68.0 0.5 copy.12
Async XLA Ops:
  66.4 1.6 %copy-start = (f32[1,8]{1,0:T(1,128)S(1)}, f32[1,8]{1,0:T(1,128)}, u32[]{:S(2)}) copy-start(f32[1,8]{1,0:T(1,128)} %get-tuple-element.5) | copy-start | bytes 100

commit v3 on v1

--- a/solution.py
+++ b/solution.py
@@ -15,9 +15,13 @@
 CAPS = 16
 ZS = 16
 ROWS = 16
-CHUNK = 32
+CHUNK = 64
 CHUNKS = K // CHUNK
+GANG = CHUNK // 8
 STEPS = CHUNKS + CAPS - 1
+RUN = STEPS + 1
+ORDER = sorted(range(1, CAPS), key=lambda d: -sum(min(x, 4 - x) for x in (d // 4, d % 4)))
+FAR = sorted(range(1, ZS), key=lambda d: -min(d, ZS - d))
 GROUPS = K // 8
 LINES = GROUPS + 8 * (CAPS - 1)
 SHIFT = 8 * (CAPS - 1)
@@ -35,12 +39,13 @@
 
 
 def kernel(
-    exit_ref, demand_ref, start_ref, mass_ref, survive_ref, trans_ref, install_ref,
+    exit_ref, demand_ref, start_hbm, mass_hbm, survive_hbm, trans_hbm, install_hbm,
     value_ref, rel_ref,
     forward, heard, heights, lines, table, jumps, table_s, jumps_s,
     reached, folded, reply, best, part, parts, root, pair, both, roots,
+    mass_ref, survive_ref, trans_ref, install_ref,
     fwd_send, fwd_recv, rep_send, rep_recv, par_send, par_recv, pair_send, pair_recv,
-    root_send, root_recv, table_sem,
+    root_send, root_recv, table_sem, load_sem,
 ):
     me = lax.axis_index("cap")
     sec = lax.axis_index("sector")
@@ -48,21 +53,36 @@
     level = sec // 2
     partner = sec + 1 - 2 * core
 
+    row, column = me // 4, lax.rem(me, 4)
+
+    def peer_of(d):
+        return 4 * lax.rem(row + d // 4, 4) + lax.rem(column + d % 4, 4)
+
+    def source_of(d):
+        return 4 * lax.rem(row + 4 - d // 4, 4) + lax.rem(column + 4 - d % 4, 4)
+
     def cap_at(d):
-        return {"cap": lax.rem(me + d, CAPS)}
+        return {"cap": peer_of(d)}
 
     def level_at(d):
         return {"sector": 2 * lax.rem(level + d, ZS) + core}
 
     barrier = pltpu.get_barrier_semaphore()
 
-    def greet(d, c):
+    for d in ORDER:
         pl.semaphore_signal(barrier, inc=1, device_id=cap_at(d))
+    for d in FAR:
         pl.semaphore_signal(barrier, inc=1, device_id=level_at(d))
-        return c
-
-    lax.fori_loop(1, CAPS, greet, 0)
     pl.semaphore_signal(barrier, inc=1, device_id={"sector": partner})
+
+    loads = [
+        pltpu.make_async_copy(source, target, load_sem.at[i])
+        for i, (source, target) in enumerate((
+            (start_hbm, value_ref), (mass_hbm, mass_ref), (survive_hbm, survive_ref),
+            (trans_hbm, trans_ref), (install_hbm, install_ref)))
+    ]
+    for load in loads:
+        load.start()
 
     capital_all = capital_of(iota((CAPS, 128), 0) * 128 + iota((CAPS, 128), 1))
     half = 0.8 * capital_all
@@ -81,18 +101,17 @@
     log_cap = math.log(0.2) + LOG10 * place.astype(jnp.float32) / (K - 1)
     log_prod = -0.5 + iota((Z, 128), 0).astype(jnp.float32) / (Z - 1)
     output = jnp.exp(log_prod + 0.6 * log_cap)
-    install = install_ref[...]
     lane = iota((ROWS, 128), 1)
     lane_f = lane.astype(jnp.float32)
 
     def fwd_copy(sweep, d):
-        peer = lax.rem(me + d, CAPS)
+        peer = peer_of(d)
         return pltpu.make_async_remote_copy(
             forward.at[sweep, peer], heard.at[sweep, me], fwd_send.at[sweep, d], fwd_recv.at[sweep, d],
             device_id=cap_at(d))
 
     def rep_copy(sweep, d):
-        peer = lax.rem(me + d, CAPS)
+        peer = peer_of(d)
         return pltpu.make_async_remote_copy(
             reply.at[sweep, peer], best.at[sweep, me], rep_send.at[sweep, d], rep_recv.at[sweep, d],
             device_id=cap_at(d))
@@ -108,18 +127,16 @@
             device_id=level_at(d))
 
     def start_all(copy, sweep):
-        def one(d, c):
+        for d in ORDER:
             copy(sweep, d).start()
-            return c
-        lax.fori_loop(1, CAPS, one, 0)
 
     def wait_all(copy, sweep):
-        def one(d, c):
+        for d in ORDER:
             copy(sweep, d).wait()
-            return c
-        lax.fori_loop(1, CAPS, one, 0)
-
-    value_ref[...] = start_ref[...]
+
+    for load in loads:
+        load.wait()
+    install = install_ref[...]
 
     def sweep_body(sweep, carry):
         sums = []
@@ -135,7 +152,9 @@
             ahead = 0.9 * expect - install
             forward[sweep, 2 * s] = ahead[:ROWS]
             forward[sweep, 2 * s + 1] = ahead[ROWS:]
-        part[sweep] = jnp.concatenate(sums, axis=0)
+        sums = jnp.sum(jnp.concatenate(sums, axis=0), axis=1, keepdims=True)
+        diagonal = iota((SEC, 128), 0) == iota((SEC, 128), 1)
+        part[sweep] = jnp.sum(jnp.where(diagonal, sums, 0.0), axis=0, keepdims=True)
 
         @pl.when(sweep == 0)
         def _():
@@ -146,7 +165,7 @@
         heard[sweep, me] = forward[sweep, me]
         parts[sweep, me] = part[sweep]
         wait_all(par_copy, sweep)
-        whole = jnp.sum(jnp.sum(parts[sweep], axis=0), axis=1, keepdims=True)
+        whole = jnp.sum(jnp.where(diagonal, jnp.sum(parts[sweep], axis=0), 0.0), axis=1, keepdims=True)
         supply = 1.0 + jnp.broadcast_to(whole, (SEC, 128)) / (Z * K)
         demand = jnp.zeros((SEC, 128), jnp.float32)
         for s in range(SEC):
@@ -157,14 +176,8 @@
             root.at[sweep], pair.at[sweep], pair_send.at[sweep], pair_recv.at[sweep],
             device_id={"sector": partner})
         to_pair.start()
-        to_pair.wait()
-        both[sweep] = root[sweep] + pair[sweep]
-        start_all(root_copy, sweep)
-        roots[sweep, level] = both[sweep]
-
-        wait_all(fwd_copy, sweep)
-
-        def spread(i, c):
+
+        def spread(i):
             rows = [heard[sweep, i] + 0.8 * capital_of(i * 128 + iota((1, 128), 1))]
             for bit in (64, 32, 16, 8):
                 high = (lane // bit) % 2 == 1
@@ -175,9 +188,16 @@
                 rows = wide
             for g in range(16):
                 heights[16 * i + g] = rows[g]
-            return c
-
-        lax.fori_loop(0, CAPS, spread, 0)
+
+        spread(me)
+        for d in ORDER:
+            fwd_copy(sweep, d).wait()
+            spread(source_of(d))
+        to_pair.wait()
+        both[sweep] = root[sweep] + pair[sweep]
+        for d in FAR:
+            root_copy(sweep, d).start()
+        roots[sweep, level] = both[sweep]
 
         tall = heard[sweep] + half[:, None, :]
         source = lax.broadcasted_iota(jnp.int32, (CAPS, ROWS, 128), 0).astype(jnp.float32)
@@ -199,12 +219,12 @@
             first = chunks[b - 1] + float(b)
             block = block + jnp.where(first <= lane_f, 1.0, 0.0)
             jump = jnp.where(first == lane_f, NEG, jump)
-        group = 4.0 * (lane_f - block)
+        group = float(GANG) * (lane_f - block)
         line = group - 8.0 * block + float(SHIFT)
         for b in range(CAPS):
             group = jnp.where(lane == ENDS + b, chunks[b] + float(b), group)
-        table[:ROWS] = jnp.clip(group.astype(jnp.int32), 0, jnp.where(lane < ENDS, GROUPS - 4, STEPS - 1))
-        table[ROWS:] = jnp.clip(line.astype(jnp.int32), 0, LINES - 4)
+        table[:ROWS] = jnp.clip(group.astype(jnp.int32), 0, jnp.where(lane < ENDS, GROUPS - GANG, STEPS - 1))
+        table[ROWS:] = jnp.clip(line.astype(jnp.int32), 0, LINES - GANG)
         jumps[...] = jump
         to_table = pltpu.make_async_copy(table, table_s, table_sem.at[0])
         to_jumps = pltpu.make_async_copy(jumps, jumps_s, table_sem.at[1])
@@ -216,22 +236,21 @@
         def step(t, accs):
             out = []
             for r in range(ROWS):
-                at_height = jnp.clip(table_s[r, t], 0, GROUPS - 4)
-                at_line = jnp.clip(table_s[ROWS + r, t], 0, LINES - 4)
-                value = heights[pl.ds(at_height, 4), r:r + 1, :] - lines[pl.ds(at_line, 4)]
+                value = heights[pl.ds(table_s[r, t], GANG), r:r + 1, :] - lines[pl.ds(table_s[ROWS + r, t], GANG)]
                 acc = jnp.maximum(jnp.max(value, axis=0), accs[r] + jumps_s[r, t])
                 reached[r, t] = acc
                 out.append(acc)
             return tuple(out)
 
-        lax.fori_loop(0, STEPS, step, tuple(jnp.full((8, 128), NEG, jnp.float32) for _ in range(ROWS)))
+        accs = tuple(jnp.full((8, 128), NEG, jnp.float32) for _ in range(ROWS))
+        lax.fori_loop(0, RUN, step, accs, unroll=2)
 
         for h in range(2):
             odd = iota((ROWS * 8, 128), 1)
             tops = []
             for p in range(8):
                 tops.append(jnp.concatenate(
-                    [reached[r, jnp.clip(table_s[r, ENDS + 8 * h + p], 0, STEPS - 1)] for r in range(ROWS)], axis=0))
+                    [reached[r, table_s[r, ENDS + 8 * h + p]] for r in range(ROWS)], axis=0))
             for bit in (4, 2, 1):
                 high = (odd // bit) % 2 == 1
                 less = []
@@ -255,7 +274,8 @@
                 reply[sweep, 8 * h + p] = ways[p]
         start_all(rep_copy, sweep)
         best[sweep, me] = reply[sweep, me]
-        wait_all(root_copy, sweep)
+        for d in FAR:
+            root_copy(sweep, d).wait()
         root_sum = jnp.sum(roots[sweep], axis=0)
         price_index = root_sum / (SEC * 2 * ZS)
         price_index = price_index * price_index
@@ -269,7 +289,7 @@
                 rows = slice(h * ROWS, (h + 1) * ROWS)
                 live = (survive_ref[s, rows] == 1) & (iota((ROWS, 128), 0) + h * ROWS >= exit_ref[s])
                 value_ref[s, rows] = jnp.where(live, relative[s:s + 1] * output[rows] + gain, scrap)
-        flat = jnp.where(iota((SEC, 128), 0) == iota((SEC, 128), 1), relative, 0.0)
+        flat = jnp.where(diagonal, relative, 0.0)
         rel_ref[...] = jnp.sum(flat, axis=0, keepdims=True)[:, :SEC]
         return carry
 
@@ -284,7 +304,7 @@
     values, relative = pl.pallas_call(
         kernel,
         out_shape=(jax.ShapeDtypeStruct((SEC, Z, 128), f32), jax.ShapeDtypeStruct((1, SEC), f32)),
-        in_specs=[smem, smem, vmem, vmem, vmem, vmem, vmem],
+        in_specs=[smem, smem] + [pl.BlockSpec(memory_space=pl.ANY)] * 5,
         out_specs=(vmem, vmem),
         scratch_shapes=[
             pltpu.VMEM((SWEEPS, CAPS, ROWS, 128), f32),
@@ -295,22 +315,26 @@
             pltpu.VMEM((ROWS, 128), f32),
             pltpu.SMEM((2 * ROWS, 128), jnp.int32),
             pltpu.SMEM((ROWS, 128), f32),
-            pltpu.VMEM((ROWS, STEPS, 8, 128), f32),
+            pltpu.VMEM((ROWS, RUN, 8, 128), f32),
             pltpu.VMEM((2, ROWS, 8, 128), f32),
             pltpu.VMEM((SWEEPS, CAPS, ROWS, 128), f32),
             pltpu.VMEM((SWEEPS, CAPS, ROWS, 128), f32),
-            pltpu.VMEM((SWEEPS, SEC, 128), f32),
-            pltpu.VMEM((SWEEPS, CAPS, SEC, 128), f32),
+            pltpu.VMEM((SWEEPS, 1, 128), f32),
+            pltpu.VMEM((SWEEPS, CAPS, 1, 128), f32),
             pltpu.VMEM((SWEEPS, 1, 128), f32),
             pltpu.VMEM((SWEEPS, 1, 128), f32),
             pltpu.VMEM((SWEEPS, 1, 128), f32),
             pltpu.VMEM((SWEEPS, ZS, 1, 128), f32),
+            pltpu.VMEM((SEC, Z, 128), f32),
+            pltpu.VMEM((SEC, Z, 128), jnp.int32),
+            pltpu.VMEM((Z, Z), f32),
+            pltpu.VMEM((1, 128), f32),
             dma((SWEEPS, CAPS)), dma((SWEEPS, CAPS)), dma((SWEEPS, CAPS)), dma((SWEEPS, CAPS)),
             dma((SWEEPS, CAPS)), dma((SWEEPS, CAPS)), dma((SWEEPS,)), dma((SWEEPS,)),
-            dma((SWEEPS, ZS)), dma((SWEEPS, ZS)), dma((2,)),
+            dma((SWEEPS, ZS)), dma((SWEEPS, ZS)), dma((2,)), dma((5,)),
         ],
         compiler_params=pltpu.CompilerParams(
-            collective_id=0, has_side_effects=True, vmem_limit_bytes=40 << 20),
+            collective_id=0, has_side_effects=True, vmem_limit_bytes=60 << 20),
     )(exit_index, demand, start_value, firm_mass, survive, transition, install_cost.reshape(1, 128))
     return values, relative.reshape(SEC)
 

time: 78.3 us -> 62.8 us (0.80)
  the two profiles are of different devices: /device:TPU:1 before, /device:TPU:2 now
where the time goes in v3:
time: 62.8 us; the launch traced here: 62.6 us
  Pallas kernels  59.9 us (95%)
  local copies, waits for them, and re-layouts  2.08 us (3%)
  between operations  0.65 us (1%)
    pallas_call x1, Pallas kernels, on_device(): pl.pallas_call(kernel, out_shape=(jax.ShapeDtypeStruct((SEC, Z, 128), f32...  59.9 us
    unnamed x4, local copies, waits for them, and re-layouts  2.08 us

profile of v3, /device:TPU:2, one launch (start us, length us, event | category | flops | bytes accessed | tf_op | source)
XLA Modules:
  0.0 62.6 jit_solution(9574787135769222909)
XLA Ops:
  0.6 59.9 %shard_map.86 = (f32[8,32,128]{2,1,0:T(8,128)}, f32[1,8]{1,0:T(1,128)}) custom-call(s32[8]{0:T(128)} %exit_ref.1, f32[8]{0:T(128)} %demand_ref.1, f32[8,32,128]{2,1,0:T(8,128)} %start_hbm.1, f32[8,32,128]{2,1,0:T(8,128)} %mass_hbm.1, s32[8,32,128]{2,1,0:T(8,128)} %survive_hbm.1, f32[32,32]{1,0:T(8,128)} %trans_hbm.1, f32[1,128]{1,0:T(1,128)} %bitcast.2), custom_call_target="tpu_custom_call" | custom-call | tf_op jit(solution)/shard_map/pallas_call | solution.py:304
  60.5 0.0 copy-start
  60.5 1.6 %copy.11 = f32[8,32,128]{2,1,0:T(8,128)} copy(f32[8,32,128]{2,1,0:T(8,128)} %get-tuple-element.8) | data formatting | bytes 262144
  62.1 0.0 copy-done
  62.1 0.5 copy.12
Async XLA Ops:
  60.5 1.6 %copy-start = (f32[1,8]{1,0:T(1,128)S(1)}, f32[1,8]{1,0:T(1,128)}, u32[]{:S(2)}) copy-start(f32[1,8]{1,0:T(1,128)} %get-tuple-element.5) | copy-start | bytes 100

commit v4 on v3

--- a/solution.py
+++ b/solution.py
@@ -21,6 +21,7 @@
 STEPS = CHUNKS + CAPS - 1
 RUN = STEPS + 1
 ORDER = sorted(range(1, CAPS), key=lambda d: -sum(min(x, 4 - x) for x in (d // 4, d % 4)))
+LATE = ORDER[7:]
 FAR = sorted(range(1, ZS), key=lambda d: -min(d, ZS - d))
 GROUPS = K // 8
 LINES = GROUPS + 8 * (CAPS - 1)
@@ -192,7 +193,8 @@
         spread(me)
         for d in ORDER:
             fwd_copy(sweep, d).wait()
-            spread(source_of(d))
+            if d not in LATE:
+                spread(source_of(d))
         to_pair.wait()
         both[sweep] = root[sweep] + pair[sweep]
         for d in FAR:
@@ -230,6 +232,8 @@
         to_jumps = pltpu.make_async_copy(jumps, jumps_s, table_sem.at[1])
         to_table.start()
         to_jumps.start()
+        for d in LATE:
+            spread(source_of(d))
         to_table.wait()
         to_jumps.wait()
 
@@ -245,12 +249,13 @@
         accs = tuple(jnp.full((8, 128), NEG, jnp.float32) for _ in range(ROWS))
         lax.fori_loop(0, RUN, step, accs, unroll=2)
 
-        for h in range(2):
+        for h in (1, 0):
             odd = iota((ROWS * 8, 128), 1)
             tops = []
-            for p in range(8):
+            group = range(8 * h, 8 * h + 8)
+            for d in group:
                 tops.append(jnp.concatenate(
-                    [reached[r, table_s[r, ENDS + 8 * h + p]] for r in range(ROWS)], axis=0))
+                    [reached[r, table_s[r, ENDS + peer_of(d)]] for r in range(ROWS)], axis=0))
             for bit in (4, 2, 1):
                 high = (odd // bit) % 2 == 1
                 less = []
@@ -270,9 +275,11 @@
                         x, y = ways[q], ways[q + bit]
                         ways[q] = jnp.where(high, pltpu.roll(y, bit, 1), x)
                         ways[q + bit] = jnp.where(high, y, pltpu.roll(x, 128 - bit, 1))
-            for p in range(8):
-                reply[sweep, 8 * h + p] = ways[p]
-        start_all(rep_copy, sweep)
+            for p, d in enumerate(group):
+                reply[sweep, peer_of(d)] = ways[p]
+            for d in ORDER:
+                if d in group:
+                    rep_copy(sweep, d).start()
         best[sweep, me] = reply[sweep, me]
         for d in FAR:
             root_copy(sweep, d).wait()
@@ -304,7 +311,7 @@
     values, relative = pl.pallas_call(
         kernel,
         out_shape=(jax.ShapeDtypeStruct((SEC, Z, 128), f32), jax.ShapeDtypeStruct((1, SEC), f32)),
-        in_specs=[smem, smem] + [pl.BlockSpec(memory_space=pl.ANY)] * 5,
+        in_specs=[smem, smem] + [pl.BlockSpec(memory_space=pltpu.HBM)] * 5,
         out_specs=(vmem, vmem),
         scratch_shapes=[
             pltpu.VMEM((SWEEPS, CAPS, ROWS, 128), f32),
@@ -334,8 +341,8 @@
             dma((SWEEPS, ZS)), dma((SWEEPS, ZS)), dma((2,)), dma((5,)),
         ],
         compiler_params=pltpu.CompilerParams(
-            collective_id=0, has_side_effects=True, vmem_limit_bytes=60 << 20),
-    )(exit_index, demand, start_value, firm_mass, survive, transition, install_cost.reshape(1, 128))
+            collective_id=0, has_side_effects=True, vmem_limit_bytes=(40 << 20)),
+    )(exit_index, demand, *(pltpu.with_memory_space_constraint(x, pltpu.HBM) for x in (start_value, firm_mass, survive, transition, install_cost.reshape(1, 128))))
     return values, relative.reshape(SEC)
 
 

time: 62.8 us -> 57.2 us (0.911)
  the two profiles are of different devices: /device:TPU:2 before, /device:TPU:1 now
where the time goes in v4:
time: 57.2 us; the launch traced here: 56.6 us
  Pallas kernels  54.1 us (95%)
  local copies, waits for them, and re-layouts  1.82 us (3%)
  between operations  0.66 us (1%)
    pallas_call x1, Pallas kernels, on_device(): pl.pallas_call(kernel, out_shape=(jax.ShapeDtypeStruct((SEC, Z, 128), f32...  54.1 us
    unnamed x6, local copies, waits for them, and re-layouts  1.82 us

profile of v4, /device:TPU:1, one launch (start us, length us, event | category | flops | bytes accessed | tf_op | source)
XLA Modules:
  0.0 56.6 jit_solution(9043541055472695355)
XLA Ops:
  0.6 0.0 copy-start.1
  0.6 0.0 copy-start
  0.7 0.6 %copy-done.1 = f32[8]{0:T(128)S(1)} copy-done((f32[8]{0:T(128)S(1)}, f32[8]{0:T(128)}, u32[]{:S(2)}) %copy-start.1) | copy-done | bytes 56
  1.3 0.0 copy-done
  1.3 54.1 %shard_map.86 = (f32[8,32,128]{2,1,0:T(8,128)S(1)}, f32[1,8]{1,0:T(1,128)S(1)}) custom-call(s32[8]{0:T(128)S(1)} %copy-done, f32[8]{0:T(128)S(1)} %copy-done.1, f32[8,32,128]{2,1,0:T(8,128)} %start_hbm.1, f32[8,32,128]{2,1,0:T(8,128)} %mass_hbm.1, s32[8,32,128]{2,1,0:T(8,128)} %survive_hbm.1, f32[32,32]{1,0:T(8,128)} %trans_hbm.1, f32[1,128]{1,0:T(1,128)} %bitcast.3), custom_call_target="tpu_custom_call" | custom-call | tf_op jit(solution)/shard_map/pallas_call | solution.py:311
  55.4 0.7 %copy.11 = f32[8,32,128]{2,1,0:T(8,128)} copy(f32[8,32,128]{2,1,0:T(8,128)S(1)} %get-tuple-element.8) | data formatting | bytes 262144
  56.1 0.5 copy.12
Async XLA Ops:
  0.6 0.7 %copy-start.1 = (f32[8]{0:T(128)S(1)}, f32[8]{0:T(128)}, u32[]{:S(2)}) copy-start(f32[8]{0:T(128)} %demand_ref.1) | copy-start | bytes 100
  0.6 0.7 %copy-start = (s32[8]{0:T(128)S(1)}, s32[8]{0:T(128)}, u32[]{:S(2)}) copy-start(s32[8]{0:T(128)} %exit_ref.1) | copy-start | bytes 100

commit v5 on v4

--- a/solution.py
+++ b/solution.py
@@ -21,12 +21,12 @@
 STEPS = CHUNKS + CAPS - 1
 RUN = STEPS + 1
 ORDER = sorted(range(1, CAPS), key=lambda d: -sum(min(x, 4 - x) for x in (d // 4, d % 4)))
-LATE = ORDER[7:]
 FAR = sorted(range(1, ZS), key=lambda d: -min(d, ZS - d))
 GROUPS = K // 8
 LINES = GROUPS + 8 * (CAPS - 1)
 SHIFT = 8 * (CAPS - 1)
-ENDS = 96
+ENDS = 48
+LINE_AT = 64
 NEG = -1e30
 LOG10 = float(np.log(np.float32(10.0)))
 
@@ -190,16 +190,9 @@
             for g in range(16):
                 heights[16 * i + g] = rows[g]
 
-        spread(me)
-        for d in ORDER:
-            fwd_copy(sweep, d).wait()
-            if d not in LATE:
-                spread(source_of(d))
+        wait_all(fwd_copy, sweep)
         to_pair.wait()
         both[sweep] = root[sweep] + pair[sweep]
-        for d in FAR:
-            root_copy(sweep, d).start()
-        roots[sweep, level] = both[sweep]
 
         tall = heard[sweep] + half[:, None, :]
         source = lax.broadcasted_iota(jnp.int32, (CAPS, ROWS, 128), 0).astype(jnp.float32)
@@ -217,22 +210,27 @@
         chunks.append(jnp.full((ROWS, 128), float(CHUNKS - 1), jnp.float32))
         block = jnp.zeros((ROWS, 128), jnp.float32)
         jump = jnp.zeros((ROWS, 128), jnp.float32)
+        time = lane_f - jnp.where(lane < LINE_AT, 0.0, float(LINE_AT))
         for b in range(1, CAPS):
             first = chunks[b - 1] + float(b)
-            block = block + jnp.where(first <= lane_f, 1.0, 0.0)
-            jump = jnp.where(first == lane_f, NEG, jump)
-        group = float(GANG) * (lane_f - block)
-        line = group - 8.0 * block + float(SHIFT)
+            block = block + jnp.where(first <= time, 1.0, 0.0)
+            jump = jnp.where(first == time, NEG, jump)
+        entry = float(GANG) * (time - block)
+        entry = entry + jnp.where(lane < LINE_AT, 0.0, float(SHIFT) - 8.0 * block)
         for b in range(CAPS):
-            group = jnp.where(lane == ENDS + b, chunks[b] + float(b), group)
-        table[:ROWS] = jnp.clip(group.astype(jnp.int32), 0, jnp.where(lane < ENDS, GROUPS - GANG, STEPS - 1))
-        table[ROWS:] = jnp.clip(line.astype(jnp.int32), 0, LINES - GANG)
+            entry = jnp.where(lane == ENDS + b, chunks[b] + float(b), entry)
+        limit = jnp.where(lane < ENDS, GROUPS - GANG, jnp.where(lane < LINE_AT, STEPS - 1, LINES - GANG))
+        table[...] = jnp.clip(entry.astype(jnp.int32), 0, limit)
         jumps[...] = jump
         to_table = pltpu.make_async_copy(table, table_s, table_sem.at[0])
         to_jumps = pltpu.make_async_copy(jumps, jumps_s, table_sem.at[1])
         to_table.start()
         to_jumps.start()
-        for d in LATE:
+        for d in FAR:
+            root_copy(sweep, d).start()
+        roots[sweep, level] = both[sweep]
+        spread(me)
+        for d in ORDER:
             spread(source_of(d))
         to_table.wait()
         to_jumps.wait()
@@ -240,14 +238,14 @@
         def step(t, accs):
             out = []
             for r in range(ROWS):
-                value = heights[pl.ds(table_s[r, t], GANG), r:r + 1, :] - lines[pl.ds(table_s[ROWS + r, t], GANG)]
+                value = heights[pl.ds(table_s[r, t], GANG), r:r + 1, :] - lines[pl.ds(table_s[r, LINE_AT + t], GANG)]
                 acc = jnp.maximum(jnp.max(value, axis=0), accs[r] + jumps_s[r, t])
                 reached[r, t] = acc
                 out.append(acc)
             return tuple(out)
 
         accs = tuple(jnp.full((8, 128), NEG, jnp.float32) for _ in range(ROWS))
-        lax.fori_loop(0, RUN, step, accs, unroll=2)
+        lax.fori_loop(0, RUN, step, accs, unroll=4)
 
         for h in (1, 0):
             odd = iota((ROWS * 8, 128), 1)
@@ -318,9 +316,9 @@
             pltpu.VMEM((SWEEPS, CAPS, ROWS, 128), f32),
             pltpu.VMEM((GROUPS, ROWS, 128), f32),
             pltpu.VMEM((LINES, 8, 128), f32),
-            pltpu.VMEM((2 * ROWS, 128), jnp.int32),
+            pltpu.VMEM((ROWS, 128), jnp.int32),
             pltpu.VMEM((ROWS, 128), f32),
-            pltpu.SMEM((2 * ROWS, 128), jnp.int32),
+            pltpu.SMEM((ROWS, 128), jnp.int32),
             pltpu.SMEM((ROWS, 128), f32),
             pltpu.VMEM((ROWS, RUN, 8, 128), f32),
             pltpu.VMEM((2, ROWS, 8, 128), f32),

time: 57.2 us -> 54.5 us (0.953)
  Pallas kernels: 54.1 us -> 51.9 us
    pallas_call x1, Pallas kernels: 54.1 us -> 51.9 us  [on_device(): pl.pallas_call(kernel, out_shape=(jax.ShapeDtypeStruct((SEC, Z, 128), f32...]
where the time goes in v5:
time: 54.5 us; the launch traced here: 54.4 us
  Pallas kernels  51.9 us (95%)
  local copies, waits for them, and re-layouts  1.82 us (3%)
  between operations  0.66 us (1%)
    pallas_call x1, Pallas kernels, on_device(): pl.pallas_call(kernel, out_shape=(jax.ShapeDtypeStruct((SEC, Z, 128), f32...  51.9 us
    unnamed x6, local copies, waits for them, and re-layouts  1.82 us

profile of v5, /device:TPU:1, one launch (start us, length us, event | category | flops | bytes accessed | tf_op | source)
XLA Modules:
  0.0 54.4 jit_solution(7873007762543149248)
XLA Ops:
  0.6 0.0 copy-start.1
  0.6 0.0 copy-start
  0.7 0.6 %copy-done.1 = f32[8]{0:T(128)S(1)} copy-done((f32[8]{0:T(128)S(1)}, f32[8]{0:T(128)}, u32[]{:S(2)}) %copy-start.1) | copy-done | bytes 56
  1.3 0.0 copy-done
  1.3 51.9 %shard_map.86 = (f32[8,32,128]{2,1,0:T(8,128)S(1)}, f32[1,8]{1,0:T(1,128)S(1)}) custom-call(s32[8]{0:T(128)S(1)} %copy-done, f32[8]{0:T(128)S(1)} %copy-done.1, f32[8,32,128]{2,1,0:T(8,128)} %start_hbm.1, f32[8,32,128]{2,1,0:T(8,128)} %mass_hbm.1, s32[8,32,128]{2,1,0:T(8,128)} %survive_hbm.1, f32[32,32]{1,0:T(8,128)} %trans_hbm.1, f32[1,128]{1,0:T(1,128)} %bitcast.3), custom_call_target="tpu_custom_call" | custom-call | tf_op jit(solution)/shard_map/pallas_call | solution.py:309
  53.2 0.7 %copy.11 = f32[8,32,128]{2,1,0:T(8,128)} copy(f32[8,32,128]{2,1,0:T(8,128)S(1)} %get-tuple-element.8) | data formatting | bytes 262144
  53.9 0.5 copy.12
Async XLA Ops:
  0.6 0.7 %copy-start.1 = (f32[8]{0:T(128)S(1)}, f32[8]{0:T(128)}, u32[]{:S(2)}) copy-start(f32[8]{0:T(128)} %demand_ref.1) | copy-start | bytes 100
  0.6 0.7 %copy-start = (s32[8]{0:T(128)S(1)}, s32[8]{0:T(128)}, u32[]{:S(2)}) copy-start(s32[8]{0:T(128)} %exit_ref.1) | copy-start | bytes 100

commit v6 on v5

--- a/solution.py
+++ b/solution.py
@@ -165,19 +165,6 @@
         start_all(fwd_copy, sweep)
         heard[sweep, me] = forward[sweep, me]
         parts[sweep, me] = part[sweep]
-        wait_all(par_copy, sweep)
-        whole = jnp.sum(jnp.where(diagonal, jnp.sum(parts[sweep], axis=0), 0.0), axis=1, keepdims=True)
-        supply = 1.0 + jnp.broadcast_to(whole, (SEC, 128)) / (Z * K)
-        demand = jnp.zeros((SEC, 128), jnp.float32)
-        for s in range(SEC):
-            demand = jnp.where(iota((SEC, 128), 0) == s, demand_ref[s], demand)
-        prices = jnp.sqrt(demand / supply)
-        root[sweep] = jnp.sum(jnp.sqrt(prices), axis=0, keepdims=True)
-        to_pair = pltpu.make_async_remote_copy(
-            root.at[sweep], pair.at[sweep], pair_send.at[sweep], pair_recv.at[sweep],
-            device_id={"sector": partner})
-        to_pair.start()
-
         def spread(i):
             rows = [heard[sweep, i] + 0.8 * capital_of(i * 128 + iota((1, 128), 1))]
             for bit in (64, 32, 16, 8):
@@ -191,8 +178,6 @@
                 heights[16 * i + g] = rows[g]
 
         wait_all(fwd_copy, sweep)
-        to_pair.wait()
-        both[sweep] = root[sweep] + pair[sweep]
 
         tall = heard[sweep] + half[:, None, :]
         source = lax.broadcasted_iota(jnp.int32, (CAPS, ROWS, 128), 0).astype(jnp.float32)
@@ -226,12 +211,26 @@
         to_jumps = pltpu.make_async_copy(jumps, jumps_s, table_sem.at[1])
         to_table.start()
         to_jumps.start()
+        wait_all(par_copy, sweep)
+        whole = jnp.sum(jnp.where(diagonal, jnp.sum(parts[sweep], axis=0), 0.0), axis=1, keepdims=True)
+        supply = 1.0 + jnp.broadcast_to(whole, (SEC, 128)) / (Z * K)
+        demand = jnp.zeros((SEC, 128), jnp.float32)
+        for s in range(SEC):
+            demand = jnp.where(iota((SEC, 128), 0) == s, demand_ref[s], demand)
+        prices = jnp.sqrt(demand / supply)
+        root[sweep] = jnp.sum(jnp.sqrt(prices), axis=0, keepdims=True)
+        to_pair = pltpu.make_async_remote_copy(
+            root.at[sweep], pair.at[sweep], pair_send.at[sweep], pair_recv.at[sweep],
+            device_id={"sector": partner})
+        to_pair.start()
+        spread(me)
+        for d in ORDER:
+            spread(source_of(d))
+        to_pair.wait()
+        both[sweep] = root[sweep] + pair[sweep]
         for d in FAR:
             root_copy(sweep, d).start()
         roots[sweep, level] = both[sweep]
-        spread(me)
-        for d in ORDER:
-            spread(source_of(d))
         to_table.wait()
         to_jumps.wait()
 

time: 54.5 us -> 53.8 us (0.987)
  Pallas kernels: 51.9 us -> 51.2 us
    pallas_call x1, Pallas kernels: 51.9 us -> 51.2 us  [on_device(): pl.pallas_call(kernel, out_shape=(jax.ShapeDtypeStruct((SEC, Z, 128), f32...]
where the time goes in v6:
time: 53.8 us; the launch traced here: 53.6 us
  Pallas kernels  51.2 us (95%)
  local copies, waits for them, and re-layouts  1.82 us (3%)
  between operations  0.66 us (1%)
    pallas_call x1, Pallas kernels, on_device(): pl.pallas_call(kernel, out_shape=(jax.ShapeDtypeStruct((SEC, Z, 128), f32...  51.2 us
    unnamed x6, local copies, waits for them, and re-layouts  1.82 us

profile of v6, /device:TPU:1, one launch (start us, length us, event | category | flops | bytes accessed | tf_op | source)
XLA Modules:
  0.0 53.6 jit_solution(9574715761680905178)
XLA Ops:
  0.6 0.0 copy-start.1
  0.6 0.0 copy-start
  0.7 0.6 %copy-done.1 = f32[8]{0:T(128)S(1)} copy-done((f32[8]{0:T(128)S(1)}, f32[8]{0:T(128)}, u32[]{:S(2)}) %copy-start.1) | copy-done | bytes 56
  1.3 0.0 copy-done
  1.3 51.2 %shard_map.86 = (f32[8,32,128]{2,1,0:T(8,128)S(1)}, f32[1,8]{1,0:T(1,128)S(1)}) custom-call(s32[8]{0:T(128)S(1)} %copy-done, f32[8]{0:T(128)S(1)} %copy-done.1, f32[8,32,128]{2,1,0:T(8,128)} %start_hbm.1, f32[8,32,128]{2,1,0:T(8,128)} %mass_hbm.1, s32[8,32,128]{2,1,0:T(8,128)} %survive_hbm.1, f32[32,32]{1,0:T(8,128)} %trans_hbm.1, f32[1,128]{1,0:T(1,128)} %bitcast.3), custom_call_target="tpu_custom_call" | custom-call | tf_op jit(solution)/shard_map/pallas_call | solution.py:308
  52.5 0.7 %copy.11 = f32[8,32,128]{2,1,0:T(8,128)} copy(f32[8,32,128]{2,1,0:T(8,128)S(1)} %get-tuple-element.8) | data formatting | bytes 262144
  53.1 0.5 copy.12
Async XLA Ops:
  0.6 0.7 %copy-start.1 = (f32[8]{0:T(128)S(1)}, f32[8]{0:T(128)}, u32[]{:S(2)}) copy-start(f32[8]{0:T(128)} %demand_ref.1) | copy-start | bytes 100
  0.6 0.7 %copy-start = (s32[8]{0:T(128)S(1)}, s32[8]{0:T(128)}, u32[]{:S(2)}) copy-start(s32[8]{0:T(128)} %exit_ref.1) | copy-start | bytes 100
